TPU v7x, 128 devices: a whole 4x4x4 slice. The times are simulated.
128 devices in a mesh: pi: 8 (over y, x_lo), pj: 16 (over x_hi, z, core).
Axes of the slice: x: 4 (x_hi: 2, x_lo: 2; x = x_hi * 2 + x_lo), y: 4, z: 4, core: 2. Of those that a mesh axis runs over, the one named last changes fastest.
Arguments:
- duo_embedding: bfloat16 [2048, 2048, 128], P('pi', 'pj'), may hold values from -12 to 12
- duo_attention_weights: float32 [128, 8], replicated, may hold values from -16 to 16
- aligned_embedding: bfloat16 [512, 64, 2048], P('pj', None, 'pi'), may hold values from -6 to 6
- aligned_scaling_weights: float32 [64], replicated, may hold values from 0.5 to 1.5
- aligned_shift_vector: float32 [64], replicated, may hold values from -3 to 3
- payload_weights: bfloat16 [64, 256], replicated, may hold values from -0.75 to 0.75
- switch_weights: bfloat16 [64, 256], replicated, may hold values from -0.75 to 0.75
- closing_weights: bfloat16 [256, 64], replicated, may hold values from -1.5 to 1.5
Outputs:
- update: bfloat16 [512, 64, 2048], P('pj', None, 'pi')
All inputs are finite; a program needn't handle non-finite values.
Results may differ from a plain program's by a relative error of at most 0.009.
Values may be sent and summed in bfloat16 or wider, within the bound.
A program may use at most 192 MiB of HBM per device.

v0:
```python
import jax
import jax.numpy as jnp
from jax import lax
from jax.sharding import Mesh
from jax.sharding import PartitionSpec as P

PI = ("pi_0", "pi_1")
EPS = 1e-05


def gathered_total(x, axis):
    return lax.all_gather(x, axis).max(0)


def over_pieces(x, axis):
    blocks = lax.all_gather(x, axis)
    return blocks.sum(axis=0)


def gathered_by_axis(x, axes, dim):
    for axis in reversed(axes):
        x = lax.all_gather(x, axis, axis=dim, tiled=True)
    return x


def rescale_embedding(inputs, axis):
    row_mean = jnp.mean(inputs, axis=axis, keepdims=True)
    centred = inputs - row_mean
    variance = jnp.mean(centred * centred, axis=axis, keepdims=True)
    return centred * lax.rsqrt(variance + EPS)


def body(
    duo_embedding,
    duo_attention_weights,
    aligned_embedding,
    aligned_scaling_weights,
    aligned_shift_vector,
    payload_weights,
    switch_weights,
    closing_weights,
):
    attender_tally = duo_attention_weights.shape[1]
    entry_tally = duo_embedding.shape[0]
    aligned_seq_tally = aligned_embedding.shape[0]
    inner_embed_size = payload_weights.shape[1]
    attender_span = inner_embed_size // attender_tally
    pair_normed = rescale_embedding(duo_embedding.astype(jnp.float32), 2)
    scores = jnp.einsum(
        "ijc,ch->hij", pair_normed, duo_attention_weights, precision=lax.Precision.HIGHEST
    )
    row_peak = gathered_total(jnp.max(scores, axis=2), "pj")
    exp_scores = jnp.exp(scores - row_peak[:, :, None]).astype(jnp.bfloat16)
    row_total = over_pieces(jnp.sum(exp_scores, axis=2, dtype=jnp.float32), "pj")
    weights_full = lax.all_gather(exp_scores, "pj", axis=2, tiled=True)
    rescaled_aligned = (
        rescale_embedding(aligned_embedding.astype(jnp.float32), 1)
        * aligned_scaling_weights[None, :, None]
        + aligned_shift_vector[None, :, None]
    ).astype(jnp.bfloat16)
    switch_share = jax.nn.sigmoid(
        jnp.einsum(
            "scn,ce->sen", rescaled_aligned, switch_weights, preferred_element_type=jnp.float32
        )
    )
    value_segment = jnp.einsum(
        "scn,ce->sen",
        gathered_by_axis(rescaled_aligned, PI, 2),
        payload_weights,
        preferred_element_type=jnp.float32,
    ).astype(jnp.bfloat16)
    piece_span = value_segment.shape[2]
    payload_each_attender = value_segment.reshape(
        aligned_seq_tally, attender_tally, attender_span, piece_span
    )
    numerator = jnp.einsum(
        "hij,shcj->shci", weights_full, payload_each_attender, preferred_element_type=jnp.float32
    )
    gate_per_head = switch_share.reshape(
        aligned_seq_tally, attender_tally, attender_span, entry_tally
    )
    averaged_result = (gate_per_head * (numerator / row_total[None, :, None, :])).astype(
        jnp.bfloat16
    )
    averaged_result = averaged_result.reshape(aligned_seq_tally, inner_embed_size, entry_tally)
    return jnp.einsum(
        "ser,ec->scr", averaged_result, closing_weights, preferred_element_type=jnp.float32
    ).astype(jnp.bfloat16)


def solution(mesh):
    finer = Mesh(mesh.devices.reshape(4, 2, mesh.shape["pj"]), ("pi_0", "pi_1", "pj"))
    placed = (P(PI, "pj", None), P(), P("pj", None, PI), P(), P(), P(), P(), P())
    return jax.shard_map(
        body, mesh=finer, in_specs=placed, out_specs=P("pj", None, PI), check_vma=False
    )
```

profile of v0, /device:TPU:1, one launch (start us, length us, event | category | flops | bytes accessed | tf_op | source)
XLA Modules:
  0.0 258.4 jit_solution(3760978803032783942)
XLA Ops:
  6.5 0.0 copy-start
  6.5 0.0 all-gather.6.cloned.1.call-start
  6.5 1.4 convert_reduce_fusion.1
  8.0 1.6 fusion.17
  9.6 2.7 %fusion.20 = bf16[32,64,256]{2,1,0:T(8,128)(2,1)} fusion(bf16[32,64,256]{2,1,0:T(8,128)(2,1)} %param.10, f32[64]{0:T(128)} %param.12, f32[64]{0:T(128)} %param.11, f32[32,256]{1,0:T(8,128)S(1)} %add_rsqrt_fusion.1, f32[32,256]{1,0:T(8,128)S(1)} %broadcast_multiply_fusion.1), kind=kLoop, calls=%fused_computation.22 | loop fusion | flops 3145728 | bytes 2163200 | tf_op jit(solution)/shard_map/convert_element_type | solution.py:60
  12.3 0.0 all-gather.6.cloned.1.call-update
  12.4 0.0 all-gather.8.cloned.1.call-start
  12.4 38.7 %all-gather.6.cloned.1.call-done = bf16[32,64,512]{2,1,0:T(8,128)(2,1)} async-done(((bf16[32,64,256]{2,1,0:T(8,128)(2,1)}), bf16[32,64,512]{2,1,0:T(8,128)(2,1)}) %all-gather.6.cloned.1.call-update) | async-done | bytes 2097168 | tf_op jit(solution)/shard_map/all_gather | solution.py:22
  51.1 0.0 all-gather.8.cloned.1.call-update
  51.1 0.0 copy-start.5
  51.2 0.0 all-gather.10.cloned.1.call-start
  51.2 0.0 slice-start
  51.2 5.8 %convert_reduce_fusion = f32[256,128]{1,0:T(8,128)S(1)} fusion(bf16[256,128,128]{2,1,0:T(8,128)(2,1)} %param.8), kind=kLoop, calls=%fused_computation.3 | loop fusion | flops 8355840 | bytes 8519680 | tf_op jit(solution)/shard_map/reduce_sum | solution.py:27
  57.0 0.0 slice-start.1
  57.1 10.9 %fusion.4 = f32[256,128]{1,0:T(8,128)S(1)} fusion(bf16[256,128,128]{2,1,0:T(8,128)(2,1)} %param.8, f32[256,128]{1,0:T(8,128)S(1)} %broadcast_multiply_fusion), kind=kLoop, calls=%fused_computation.7 | loop fusion | flops 16744448 | bytes 8650752 | tf_op jit(solution)/shard_map/reduce_sum | solution.py:29
  68.0 0.0 copy-done.5
  68.0 0.0 slice-done
  68.0 0.0 slice-done.1
  68.0 0.0 copy-start.2
  68.0 0.0 copy-start.4
  68.0 31.4 %fusion.29 = (f32[8,256]{0,1:T(8,128)S(1)}, f32[8,256,128]{2,0,1:T(8,128)S(1)}) fusion(f32[128,8]{0,1:T(8,128)S(1)} %copy-done.5, bf16[256,128,128]{2,1,0:T(8,128)(2,1)S(1)} %bitcast.39, f32[256,128]{1,0:T(8,128)S(1)} %add_rsqrt_fusion, f32[256,128]{1,0:T(8,128)S(1)} %broadcast_multiply_fusion), kind=kOutput, calls=%fused_computation.38 | convolution fusion | flops 415496192 | bytes 9711616 | tf_op jit(solution)/shard_map/ijc,ch->hij/dot_general | solution.py:49
  99.4 0.1 copy.26
  99.5 25.0 %all-gather = f32[128,256]{1,0:T(8,128)S(1)} all-gather(f32[8,256]{1,0:T(8,128)S(1)} %copy.26), channel_id=2, replica_groups=mesh['pi_0'=4,'pi_1'=2,'pj'=16] {'pj'}, dimensions={0}, use_global_device_ids=true | all-gather | bytes 139264 | tf_op jit(solution)/shard_map/all_gather | solution.py:12
  124.5 0.1 copy.27
  124.6 1.2 convert_reduce_fusion.2
  125.8 0.0 all-gather.10.cloned.1.call-update
  125.8 0.1 copy.30
  125.9 19.6 %all-gather.1 = f32[128,256]{1,0:T(8,128)S(1)} all-gather(f32[8,256]{1,0:T(8,128)S(1)} %copy.30), channel_id=3, replica_groups=mesh['pi_0'=4,'pi_1'=2,'pj'=16] {'pj'}, dimensions={0}, use_global_device_ids=true | all-gather | bytes 139264 | tf_op jit(solution)/shard_map/all_gather | solution.py:16
  145.5 0.0 copy-done.2
  145.5 0.0 copy-done.4
  145.6 5.9 %add_divide_fusion = f32[32,256,256]{1,2,0:T(8,128)} fusion(bf16[32,64,256]{2,1,0:T(8,128)(2,1)S(1)} %copy-done.2, bf16[64,256]{1,0:T(8,128)(2,1)S(1)} %copy-done.4), kind=kOutput, calls=%fused_computation.14 | convolution fusion | flops 274726912 | bytes 9469952 | tf_op jit(solution)/shard_map/scn,ce->sen/dot_general | solution.py:62
  151.5 0.0 all-gather.8.cloned.1.call-done
  151.5 0.0 copy-done
  151.5 17.4 %convolution_convert_fusion = bf16[32,2048,256]{1,2,0:T(8,128)(2,1)} fusion(bf16[32,64,2048]{2,1,0:T(8,128)(2,1)} %all-gather.8.cloned.1.call-done, bf16[64,256]{1,0:T(8,128)(2,1)S(1)} %copy-done), kind=kOutput, calls=%fused_computation.4 | convolution fusion | flops 2164260864 | bytes 41975808 | tf_op jit(solution)/shard_map/scn,ce->sen/dot_general | solution.py:66
  168.9 48.3 %all-gather.10.cloned.1.call-done = bf16[8,256,2048]{2,0,1:T(8,128)(2,1)} async-done(((bf16[8,256,128]{2,0,1:T(8,128)(2,1)}), bf16[8,256,2048]{2,0,1:T(8,128)(2,1)}) %all-gather.10.cloned.1.call-update) | async-done | bytes 8388624 | tf_op jit(solution)/shard_map/all_gather | solution.py:55
  217.2 0.0 copy-start.1
  217.2 30.2 %fusion.7 = bf16[32,8,32,256]{3,2,0,1:T(8,128)(2,1)} fusion(f32[32,8,32,256]{3,2,1,0:T(8,128)} %bitcast.42, bf16[8,256,2048,1]{2,0,1,3:T(8,128)(2,1)} %bitcast.41, bf16[32,8,32,2048]{3,2,1,0:T(8,128)(2,1)} %bitcast.37, f32[8,256]{1,0:T(8,128)S(1)} %bitcast_reduce_fusion), kind=kOutput, calls=%fused_computation.10 | convolution fusion | flops 8596226048 | bytes 54534144 | tf_op jit(solution)/shard_map/hij,shcj->shci/dot_general | solution.py:76
  247.4 0.0 copy-start.3
  247.4 2.6 %copy.32 = bf16[32,8,32,256]{3,2,1,0:T(8,128)(2,1)S(1)} copy(bf16[32,8,32,256]{3,2,0,1:T(8,128)(2,1)} %fusion.7) | data formatting | bytes 8388608 | tf_op jit(solution)/shard_map/convert_element_type | solution.py:82
  250.1 0.0 copy-done.3
  250.1 1.8 fusion.21
  251.9 0.0 copy-done.1
  (7 shorter events, 0.1 us)
Async XLA Ops:
  6.5 144.9 %copy-start = (bf16[64,256]{1,0:T(8,128)(2,1)S(1)}, bf16[64,256]{1,0:T(8,128)(2,1)}, u32[]{:S(2)}) copy-start(bf16[64,256]{1,0:T(8,128)(2,1)} %param.13) | copy-start | bytes 98308
  6.5 44.6 %all-gather.6.cloned.1.call-start = ((), (), s32[]{:S(2)}) async-start(), calls=%async_computation | async-start | bytes 3145728 | tf_op jit(solution)/shard_map/all_gather | solution.py:22
  12.4 139.1 %all-gather.8.cloned.1.call-start = ((), (), s32[]{:S(2)}) async-start(), calls=%async_computation.1 | async-start | bytes 10485760 | tf_op jit(solution)/shard_map/all_gather | solution.py:22
  51.1 16.8 %copy-start.5 = (f32[128,8]{0,1:T(8,128)S(1)}, f32[128,8]{0,1:T(8,128)}, u32[]{:S(2)}) copy-start(f32[128,8]{0,1:T(8,128)} %param.9) | copy-start | bytes 12292
  51.2 166.1 %all-gather.10.cloned.1.call-start = ((), (), s32[]{:S(2)}) async-start(), calls=%async_computation.2 | async-start | bytes 8912896 | tf_op jit(solution)/shard_map/all_gather | solution.py:55
  51.2 16.8 %slice-start = ((s8[8388608]{0:T(1024)(128)(4,1)}), s8[4194304]{0:T(1024)(128)(4,1)S(1)}, s32[]{:S(2)}) async-start(s8[8388608]{0:T(1024)(128)(4,1)} %bitcast.38), calls=%async_computation.3 | async-start | bytes 8388608
  57.0 10.9 %slice-start.1 = ((s8[8388608]{0:T(1024)(128)(4,1)}), s8[4194304]{0:T(1024)(128)(4,1)S(1)}, s32[]{:S(2)}) async-start(s8[8388608]{0:T(1024)(128)(4,1)} %bitcast.38), calls=%async_computation.4 | async-start | bytes 8388608
  68.0 77.5 %copy-start.2 = (bf16[32,64,256]{2,1,0:T(8,128)(2,1)S(1)}, bf16[32,64,256]{2,1,0:T(8,128)(2,1)}, u32[]{:S(2)}) copy-start(bf16[32,64,256]{2,1,0:T(8,128)(2,1)} %fusion.20) | copy-start | bytes 3145732
  68.0 77.5 %copy-start.4 = (bf16[64,256]{1,0:T(8,128)(2,1)S(1)}, bf16[64,256]{1,0:T(8,128)(2,1)}, u32[]{:S(2)}) copy-start(bf16[64,256]{1,0:T(8,128)(2,1)} %param.14) | copy-start | bytes 98308
  217.2 34.7 %copy-start.1 = (bf16[64,256]{1,0:T(8,128)(2,1)S(1)}, bf16[64,256]{1,0:T(8,128)(2,1)}, u32[]{:S(2)}) copy-start(bf16[64,256]{1,0:T(8,128)(2,1)} %param.13) | copy-start | bytes 98308
  247.4 2.6 %copy-start.3 = (bf16[256,64]{0,1:T(8,128)(2,1)S(1)}, bf16[256,64]{0,1:T(8,128)(2,1)}, u32[]{:S(2)}) copy-start(bf16[256,64]{0,1:T(8,128)(2,1)} %param.15) | copy-start | bytes 98308
Sparse Core Ops, SparseCore 0:
  12.5 38.5 all-gather.5
  52.8 84.0 all-gather.7
  139.2 78.0 all-gather.9
where the time goes:
time: 259 us; the launch traced here: 258 us
  waiting for transfers between devices  87.1 us (34%)
  matrix products  86.8 us (34%)
  blocking collectives  44.6 us (17%)
  other arithmetic  23.7 us (9%)
  between operations  13.3 us (5%)
  local copies, waits for them, and re-layouts  2.92 us (1%)
    all_gather x1, waiting for transfers between devices, body(): weights_full = lax.all_gather(exp_scores, 'pj', axis=2, tiled=True)  48.3 us
    all_gather x2, waiting for transfers between devices, gathered_by_axis(): x = lax.all_gather(x, axis, axis=dim, tiled=True)  38.7 us
    dot_general x1, matrix products, body(): jnp.einsum('ijc,ch->hij', pair_normed, duo_attention_weights, precision=l...  31.4 us
    dot_general x1, matrix products, body(): jnp.einsum('hij,shcj->shci', weights_full, payload_each_attender, preferr...  30.2 us
    all_gather x1, blocking collectives, gathered_total(): return lax.all_gather(x, axis).max(0)  25 us
    all_gather x1, blocking collectives, over_pieces(): blocks = lax.all_gather(x, axis)  19.6 us
    dot_general x1, matrix products, body(): jnp.einsum('scn,ce->sen', gathered_by_axis(rescaled_aligned, PI, 2), payl...  17.4 us
    reduce_sum x2, other arithmetic, rescale_embedding(): variance = jnp.mean(centred * centred, axis=axis, keepdims=True)  12.5 us
  transfers between devices with their start and end apart: 3, of which 2 were waited for; matrix products, arithmetic and copies ran while one was open for 28% of the time, Pallas kernels for 0%

commit v1 on v0

--- a/solution.py
+++ b/solution.py
@@ -52,7 +52,9 @@
     row_peak = gathered_total(jnp.max(scores, axis=2), "pj")
     exp_scores = jnp.exp(scores - row_peak[:, :, None]).astype(jnp.bfloat16)
     row_total = over_pieces(jnp.sum(exp_scores, axis=2, dtype=jnp.float32), "pj")
-    weights_full = lax.all_gather(exp_scores, "pj", axis=2, tiled=True)
+    weights_full = jnp.concatenate(
+        lax.all_to_all(jnp.stack([exp_scores] * lax.axis_size("pj")), "pj", 0, 0), axis=2
+    )
     rescaled_aligned = (
         rescale_embedding(aligned_embedding.astype(jnp.float32), 1)
         * aligned_scaling_weights[None, :, None]

time: 259 us -> 356 us (1.37)
  blocking collectives: 44.6 us -> 165 us
  waiting for transfers between devices: 87.1 us -> 38.7 us
  local copies, waits for them, and re-layouts: 2.92 us -> 33.6 us
  matrix products: 86.8 us -> 76.5 us
  starting transfers between devices: 0.08 us -> 4.83 us
    all_gather x1, blocking collectives: 19.6 us -> 140 us  [over_pieces(): blocks = lax.all_gather(x, axis)]
    all_gather x1 -> x0, waiting for transfers between devices: 48.3 us -> none  [body(): weights_full = lax.all_gather(exp_scores, 'pj', axis=2, tiled=True)]
    reshape x0 -> x2, local copies, waits for them, and re-layouts: none -> 25.3 us  [body(): jnp.concatenate(lax.all_to_all(jnp.stack([exp_scores] * lax.axis_size('pj...]
    dot_general x1, matrix products: 30.2 us -> 20.1 us  [body(): jnp.einsum('hij,shcj->shci', weights_full, payload_each_attender, preferr...]
    another operation x0 -> x1, local copies, waits for them, and re-layouts: none -> 5.3 us  [body(): jnp.stack([exp_scores] * lax.axis_size('pj'))]
    all_to_all x0 -> x1, starting transfers between devices: none -> 4.79 us  [body(): lax.all_to_all(jnp.stack([exp_scores] * lax.axis_size('pj')), 'pj', 0, 0)]
  transfers between devices with their start and end apart: 3 -> 3, of which waited for: 2 -> 1; matrix products, arithmetic and copies ran while one was open for 28% -> 24% of each run, Pallas kernels for 0% -> 0%
where the time goes in v1:
time: 356 us; the launch traced here: 355 us
  blocking collectives  165 us (46%)
  matrix products  76.5 us (21%)
  waiting for transfers between devices  38.7 us (11%)
  local copies, waits for them, and re-layouts  33.6 us (9%)
  other arithmetic  23.1 us (6%)
  between operations  13.6 us (4%)
  starting transfers between devices  4.83 us (1%)
    all_gather x1, blocking collectives, over_pieces(): blocks = lax.all_gather(x, axis)  140 us
    all_gather x2, waiting for transfers between devices, gathered_by_axis(): x = lax.all_gather(x, axis, axis=dim, tiled=True)  38.7 us
    dot_general x1, matrix products, body(): jnp.einsum('ijc,ch->hij', pair_normed, duo_attention_weights, precision=l...  31.4 us
    reshape x2, local copies, waits for them, and re-layouts, body(): jnp.concatenate(lax.all_to_all(jnp.stack([exp_scores] * lax.axis_size('pj...  25.3 us
    all_gather x1, blocking collectives, gathered_total(): return lax.all_gather(x, axis).max(0)  25 us
    dot_general x1, matrix products, body(): jnp.einsum('hij,shcj->shci', weights_full, payload_each_attender, preferr...  20.1 us
    dot_general x1, matrix products, body(): jnp.einsum('scn,ce->sen', gathered_by_axis(rescaled_aligned, PI, 2), payl...  17.3 us
    reduce_sum x2, other arithmetic, rescale_embedding(): variance = jnp.mean(centred * centred, axis=axis, keepdims=True)  12.5 us
  transfers between devices with their start and end apart: 3, of which 1 were waited for; matrix products, arithmetic and copies ran while one was open for 24% of the time, Pallas kernels for 0%

profile of v1, /device:TPU:1, one launch (start us, length us, event | category | flops | bytes accessed | tf_op | source)
XLA Modules:
  0.0 355.4 jit_solution(1562562548273707315)
XLA Ops:
  6.5 0.0 copy-start
  6.5 0.0 all-gather.5.cloned.1.call-start
  6.5 1.4 convert_reduce_fusion.1
  8.0 1.6 fusion.17
  9.6 2.7 fusion.20
  12.3 0.0 all-gather.5.cloned.1.call-update
  12.4 0.0 all-gather.7.cloned.1.call-start
  12.4 38.7 %all-gather.5.cloned.1.call-done = bf16[32,64,512]{2,1,0:T(8,128)(2,1)} async-done(((bf16[32,64,256]{2,1,0:T(8,128)(2,1)}), bf16[32,64,512]{2,1,0:T(8,128)(2,1)}) %all-gather.5.cloned.1.call-update) | async-done | bytes 2097168 | tf_op jit(solution)/shard_map/all_gather | solution.py:22
  51.1 0.0 all-gather.7.cloned.1.call-update
  51.1 0.0 slice-start
  51.2 0.0 copy-start.5
  51.2 5.8 %convert_reduce_fusion = f32[256,128]{1,0:T(8,128)S(1)} fusion(bf16[256,128,128]{2,1,0:T(8,128)(2,1)} %param.8), kind=kLoop, calls=%fused_computation.3 | loop fusion | flops 8355840 | bytes 8519680 | tf_op jit(solution)/shard_map/reduce_sum | solution.py:27
  57.0 0.0 slice-start.1
  57.0 10.9 %fusion.4 = f32[256,128]{1,0:T(8,128)S(1)} fusion(bf16[256,128,128]{2,1,0:T(8,128)(2,1)} %param.8, f32[256,128]{1,0:T(8,128)S(1)} %broadcast_multiply_fusion), kind=kLoop, calls=%fused_computation.7 | loop fusion | flops 16744448 | bytes 8650752 | tf_op jit(solution)/shard_map/reduce_sum | solution.py:29
  67.9 0.0 slice-done
  67.9 0.0 copy-done.5
  67.9 0.0 slice-done.1
  67.9 31.4 %fusion.29 = (f32[8,256]{0,1:T(8,128)S(1)}, f32[8,256,128]{2,0,1:T(8,128)S(1)}) fusion(f32[128,8]{0,1:T(8,128)S(1)} %copy-done.5, bf16[256,128,128]{2,1,0:T(8,128)(2,1)S(1)} %bitcast.46, f32[256,128]{1,0:T(8,128)S(1)} %add_rsqrt_fusion, f32[256,128]{1,0:T(8,128)S(1)} %broadcast_multiply_fusion), kind=kOutput, calls=%fused_computation.38 | convolution fusion | flops 415496192 | bytes 9711616 | tf_op jit(solution)/shard_map/ijc,ch->hij/dot_general | solution.py:49
  99.4 0.1 copy.28
  99.4 25.0 %all-gather = f32[128,256]{1,0:T(8,128)S(1)} all-gather(f32[8,256]{1,0:T(8,128)S(1)} %copy.28), channel_id=2, replica_groups=mesh['pi_0'=4,'pi_1'=2,'pj'=16] {'pj'}, dimensions={0}, use_global_device_ids=true | all-gather | bytes 139264 | tf_op jit(solution)/shard_map/all_gather | solution.py:12
  124.4 0.1 copy.29
  124.6 0.6 convert_reduce_fusion.2
  125.2 0.1 copy.30
  125.3 5.3 %stack.2 = bf16[16,8,256,128]{3,2,1,0:T(8,128)(2,1)} broadcast(bf16[8,256,128]{2,1,0:T(8,128)(2,1)S(1)} %copy.30), dimensions={1,2,3} | broadcast | bytes 8912896 | tf_op jit(solution)/shard_map/stack | solution.py:56
  130.6 0.0 copy-start.2
  130.6 0.0 copy-start.4
  130.6 4.8 %all-to-all-start = ((bf16[16,8,256,128]{3,2,1,0:T(8,128)(2,1)}), bf16[16,8,256,128]{3,2,1,0:T(8,128)(2,1)}, u32[]{:S(2)}, u32[]{:S(2)}) async-start(bf16[16,8,256,128]{3,2,1,0:T(8,128)(2,1)} %stack.2), calls=%async_computation | async-start | bytes 16777216 | tf_op jit(solution)/shard_map/all_to_all | solution.py:56
  135.4 0.1 copy.33
  135.5 140.0 %all-gather.1 = f32[128,256]{1,0:T(8,128)S(1)} all-gather(f32[8,256]{1,0:T(8,128)S(1)} %copy.33), channel_id=3, replica_groups=mesh['pi_0'=4,'pi_1'=2,'pj'=16] {'pj'}, dimensions={0}, use_global_device_ids=true | all-gather | bytes 139264 | tf_op jit(solution)/shard_map/all_gather | solution.py:16
  275.5 0.0 copy-done.2
  275.5 0.0 copy-done.4
  275.5 5.9 %add_divide_fusion = f32[32,256,256]{1,2,0:T(8,128)} fusion(bf16[32,64,256]{2,1,0:T(8,128)(2,1)S(1)} %copy-done.2, bf16[64,256]{1,0:T(8,128)(2,1)S(1)} %copy-done.4), kind=kOutput, calls=%fused_computation.14 | convolution fusion | flops 274726912 | bytes 9469952 | tf_op jit(solution)/shard_map/scn,ce->sen/dot_general | solution.py:64
  281.4 0.0 all-to-all-done
  281.4 12.0 %copy.31 = bf16[8,256,16,128]{3,2,1,0:T(8,128)(2,1)} copy(bf16[8,256,16,128]{3,1,0,2:T(8,128)(2,1)} %bitcast.9) | data formatting | bytes 16777216 | tf_op jit(solution)/shard_map/reshape | solution.py:55
  293.4 13.3 %reshape.55 = bf16[8,256,2048,1]{2,1,0,3:T(8,128)(2,1)} reshape(bf16[8,256,16,128]{3,2,1,0:T(8,128)(2,1)} %copy.31) | data formatting | bytes 16777216 | tf_op jit(solution)/shard_map/reshape | solution.py:55
  306.7 0.0 all-gather.7.cloned.1.call-done
  306.7 0.0 copy-done
  306.7 17.3 %convolution_convert_fusion = bf16[32,2048,256]{1,2,0:T(8,128)(2,1)} fusion(bf16[32,64,2048]{2,1,0:T(8,128)(2,1)} %all-gather.7.cloned.1.call-done, bf16[64,256]{1,0:T(8,128)(2,1)S(1)} %copy-done), kind=kOutput, calls=%fused_computation.4 | convolution fusion | flops 2164260864 | bytes 41975808 | tf_op jit(solution)/shard_map/scn,ce->sen/dot_general | solution.py:68
  324.0 0.0 copy-start.1
  324.0 20.1 %fusion.7 = bf16[32,8,32,256]{3,2,0,1:T(8,128)(2,1)} fusion(f32[32,8,32,256]{3,2,1,0:T(8,128)} %bitcast.48, bf16[8,256,2048,1]{2,1,0,3:T(8,128)(2,1)} %reshape.55, bf16[32,8,32,2048]{3,2,1,0:T(8,128)(2,1)} %bitcast.44, f32[8,256]{1,0:T(8,128)S(1)} %bitcast_reduce_fusion), kind=kOutput, calls=%fused_computation.10 | convolution fusion | flops 8596226048 | bytes 54534144 | tf_op jit(solution)/shard_map/hij,shcj->shci/dot_general | solution.py:78
  344.1 0.0 copy-start.3
  344.1 2.6 copy.35
  346.7 0.0 copy-done.3
  346.8 1.8 fusion.21
  348.6 0.0 copy-done.1
  (7 shorter events, 0.1 us)
Async XLA Ops:
  6.5 300.2 %copy-start = (bf16[64,256]{1,0:T(8,128)(2,1)S(1)}, bf16[64,256]{1,0:T(8,128)(2,1)}, u32[]{:S(2)}) copy-start(bf16[64,256]{1,0:T(8,128)(2,1)} %param.13) | copy-start | bytes 98308
  6.5 44.6 %all-gather.5.cloned.1.call-start = ((), (), s32[]{:S(2)}) async-start(), calls=%async_computation.1 | async-start | bytes 3145728 | tf_op jit(solution)/shard_map/all_gather | solution.py:22
  12.4 294.3 %all-gather.7.cloned.1.call-start = ((), (), s32[]{:S(2)}) async-start(), calls=%async_computation.2 | async-start | bytes 10485760 | tf_op jit(solution)/shard_map/all_gather | solution.py:22
  51.1 16.8 %slice-start = ((s8[8388608]{0:T(1024)(128)(4,1)}), s8[4194304]{0:T(1024)(128)(4,1)S(1)}, s32[]{:S(2)}) async-start(s8[8388608]{0:T(1024)(128)(4,1)} %bitcast.45), calls=%async_computation.3 | async-start | bytes 8388608
  51.2 16.8 %copy-start.5 = (f32[128,8]{0,1:T(8,128)S(1)}, f32[128,8]{0,1:T(8,128)}, u32[]{:S(2)}) copy-start(f32[128,8]{0,1:T(8,128)} %param.9) | copy-start | bytes 12292
  57.0 10.9 %slice-start.1 = ((s8[8388608]{0:T(1024)(128)(4,1)}), s8[4194304]{0:T(1024)(128)(4,1)S(1)}, s32[]{:S(2)}) async-start(s8[8388608]{0:T(1024)(128)(4,1)} %bitcast.45), calls=%async_computation.4 | async-start | bytes 8388608
  130.6 144.9 %copy-start.2 = (bf16[32,64,256]{2,1,0:T(8,128)(2,1)S(1)}, bf16[32,64,256]{2,1,0:T(8,128)(2,1)}, u32[]{:S(2)}) copy-start(bf16[32,64,256]{2,1,0:T(8,128)(2,1)} %fusion.20) | copy-start | bytes 3145732
  130.6 144.9 %copy-start.4 = (bf16[64,256]{1,0:T(8,128)(2,1)S(1)}, bf16[64,256]{1,0:T(8,128)(2,1)}, u32[]{:S(2)}) copy-start(bf16[64,256]{1,0:T(8,128)(2,1)} %param.14) | copy-start | bytes 98308
  130.6 150.8 %all-to-all-start = ((bf16[16,8,256,128]{3,2,1,0:T(8,128)(2,1)}), bf16[16,8,256,128]{3,2,1,0:T(8,128)(2,1)}, u32[]{:S(2)}, u32[]{:S(2)}) async-start(bf16[16,8,256,128]{3,2,1,0:T(8,128)(2,1)} %stack.2), calls=%async_computation | async-start | bytes 16777216 | tf_op jit(solution)/shard_map/all_to_all | solution.py:56
  324.0 24.6 %copy-start.1 = (bf16[64,256]{1,0:T(8,128)(2,1)S(1)}, bf16[64,256]{1,0:T(8,128)(2,1)}, u32[]{:S(2)}) copy-start(bf16[64,256]{1,0:T(8,128)(2,1)} %param.13) | copy-start | bytes 98308
  344.1 2.6 copy-start.3
Sparse Core Ops, SparseCore 0:
  12.5 38.5 all-gather.4
  52.8 84.0 all-gather.6
